TPU v7x, 256 devices: a 4x2x16 block of a 4x16x16 slice. The times are simulated.
256 devices in a mesh: grp: 2 (over y), slab: 16 (over z), blk: 4 (over x), sub: 2 (over core).
Axes of the slice: x: 4, y: 2, z: 16, core: 2. Of those that a mesh axis runs over, the one named last changes fastest.
The devices are a block of a 4x16x16 slice.
Arguments:
- cell_x: int32 [65536], P(('grp', 'slab', 'blk', 'sub')), parts along dimension 0, may hold values from 0 to 63
- cell_y: int32 [65536], P(('grp', 'slab', 'blk', 'sub')), parts along dimension 0, may hold values from 0 to 127
- cell_z: int32 [65536], P(('grp', 'slab', 'blk', 'sub')), parts along dimension 0, may hold values from 0 to 127
- offsets: float32 [3, 65536], P(None, ('grp', 'slab', 'blk', 'sub')), parts along dimension 1, may hold values from 0 to 1
- charge: float32 [65536], P(('grp', 'slab', 'blk', 'sub')), parts along dimension 0, may hold values from -4 to 4
- block_count: int32 [256], P(('grp', 'slab', 'blk', 'sub')), parts along dimension 0, may hold values from 0 to 256, as said below
- level_amplitude: float32 [4], replicated, may hold values from 0.5 to 2
- density: float32 [512, 256, 256], P(('grp', 'slab'), 'blk', 'sub'), parts along dimension 0, may hold values from 0.3 to 8.2
Outputs:
- field: float32 [512, 256, 256], P(('grp', 'slab'), 'blk', 'sub'), parts along dimension 0
- energy: float32 [2], P('grp'), parts along dimension 0
There are 2 independent parts, one for each index of `grp`. A program takes and returns all parts, laid end to end along the dimension named above; an argument that names none is the same for every part. Nothing has to cross between parts.
Inputs may be any that keep to these rules, and one draw needn't show every extreme that they name: `block_count`: within the 1 block of each device, blocks with a nonzero count come before blocks with count 0; some device has every block full.
All inputs are finite; a program needn't handle non-finite values.
Results may differ from a plain program's by a relative error of at most 0.0021.
Values sent between devices are 32-bit elements; how exact they have to be, the bound alone decides.
A program may use at most 64 MiB of HBM per device.

v0:
```python
import functools
import jax
import jax.numpy as jnp
from jax import lax
from jax.sharding import PartitionSpec as P

G0X = 64
G0Y = 128
G0Z = 128
FINE_X = 256
FINE_Y = 256
FINE_Z = 256
BQ = 256
spread_width = 1.25


def rows_first(arrays, axis, dims):
    turned = [jnp.moveaxis(a, dim, 0) for a, dim in zip(arrays, dims)]
    both = jnp.concatenate([t.reshape(len(t), -1) for t in turned], axis=1)
    out, at, gathered = (lax.all_gather(both, axis, axis=0, tiled=True), 0, [])
    for t, dim in zip(turned, dims):
        share = out[:, at : at + t[0].size].reshape(-1, *t.shape[1:])
        gathered.append(jnp.moveaxis(share, 0, dim))
        at += t[0].size
    return tuple(gathered)


def over_pieces(value, axis):
    return lax.all_gather(value, axis).sum(0)


def passed_along(value, axis, by):
    peers = lax.axis_size(axis)
    return lax.ppermute(value, axis, [(i, (i + by) % peers) for i in range(peers)])


def by_axis(value, axes):
    return functools.reduce(lax.psum, axes, value)


def axis_weights(shifts, base, coarse):
    position = shifts * (coarse / base)
    nodes = jnp.arange(coarse, dtype=jnp.float32)
    distance = nodes[None, :] - position[:, None]
    distance = distance - coarse * jnp.floor(distance / coarse + 0.5)
    return jnp.exp(-0.5 * (distance / spread_width) ** 2)


def placed_weights(placed, base, coarse, first, count):
    position = placed * (coarse / base)
    nodes = first.astype(jnp.float32) + jnp.arange(count, dtype=jnp.float32)
    distance = nodes[None, :] - position[:, None]
    distance = distance - coarse * jnp.floor(distance / coarse + 0.5)
    return jnp.exp(-0.5 * (distance / spread_width) ** 2)


def level_dims():
    return [
        (G0X * (4 - factor) // 4, G0Y * (4 - factor) // 4, G0Z * (4 - factor) // 4)
        for factor in range(4)
    ]


def spread_slab(totals, pieces, slab_index, slab_count):
    weighted, placed_x, placed_y, placed_z = pieces
    result = []
    for total, (dim_x, dim_y, dim_z) in zip(totals, level_dims()):
        slab_rows = dim_x // slab_count
        along_x = placed_weights(placed_x, G0X, dim_x, slab_index * slab_rows, slab_rows)
        along_y = axis_weights(placed_y, G0Y, dim_y)
        along_z = axis_weights(placed_z, G0Z, dim_z)
        planes = (
            ((weighted[:, None] * along_x)[:, :, None] * along_y[:, None, :])
            .reshape(weighted.shape[0], slab_rows * dim_y)
            .astype(jnp.bfloat16)
        )
        result.append(
            total
            + lax.dot_general(
                planes,
                along_z.astype(jnp.bfloat16),
                (((0,), (0,)), ((), ())),
                preferred_element_type=jnp.float32,
            )
        )
    return tuple(result)


def hat_matrix(fine, coarse, first_row, rows):
    fine_rows = first_row + jnp.arange(rows, dtype=jnp.int32)
    nodes = jnp.arange(coarse, dtype=jnp.int32)
    period = coarse * fine
    moved = (nodes[None, :] * fine - fine_rows[:, None] * coarse) % period
    moved = jnp.where(moved * 2 >= period, moved - period, moved)
    distance = moved.astype(jnp.float32) / fine
    return jnp.maximum(0.0, 1.0 - jnp.abs(distance))


def local_hat(fine_rows, coarse_cols, coarse):
    row_ids = jnp.arange(fine_rows, dtype=jnp.int32)
    col_ids = jnp.arange(coarse_cols, dtype=jnp.int32)
    moved = col_ids[None, :] * FINE_X - row_ids[:, None] * coarse
    distance = moved.astype(jnp.float32) / FINE_X
    return jnp.maximum(0.0, 1.0 - jnp.abs(distance))


def interpolate(mat_x, mat_y, mat_z, cube):
    highest = lax.Precision.HIGHEST
    first = jnp.einsum("ax,xyz->ayz", mat_x, cube, precision=highest)
    second = jnp.einsum("by,ayz->abz", mat_y, first, precision=highest)
    return jnp.einsum("cz,abz->abc", mat_z, second, precision=highest)


def on_device(cell_x, cell_y, cell_z, offsets, charge, block_count, level_amplitude, density):
    blocks = block_count.shape[0]
    live = (jnp.arange(BQ, dtype=jnp.int32)[None, :] < block_count[:, None]).astype(jnp.float32)
    weighted = charge.reshape(blocks, BQ) * live
    slab_count = lax.axis_size("slab")
    slab_index = lax.axis_index("slab")
    placed_x = cell_x.astype(jnp.float32) + offsets[0]
    placed_y = cell_y.astype(jnp.float32) + offsets[1]
    placed_z = cell_z.astype(jnp.float32) + offsets[2]
    flat_weighted = weighted.reshape(-1)
    begin = tuple(
        (
            jnp.zeros((dim_x // slab_count * dim_y, dim_z), jnp.float32)
            for dim_x, dim_y, dim_z in level_dims()
        )
    )
    totals = begin
    pieces = rows_first((flat_weighted, placed_x, placed_y, placed_z), "slab", (0, 0, 0, 0))
    spread_rows = pieces[0].shape[0]
    full = spread_rows // BQ

    def one_block(number, carried):
        block = tuple((lax.dynamic_slice_in_dim(array, number * BQ, BQ) for array in pieces))
        return spread_slab(carried, block, slab_index, slab_count)

    totals = lax.fori_loop(0, full, one_block, totals)
    summed = jax.tree.map(lambda part: over_pieces(part, ("blk", "sub")), totals)
    slabs = tuple(
        (
            rows.reshape(dim_x // slab_count, dim_y, dim_z)
            for rows, (dim_x, dim_y, dim_z) in zip(summed, level_dims())
        )
    )
    firsts = tuple((piece[0:1] for piece in slabs))
    after = passed_along(firsts, "slab", -1)
    rows_x, rows_y, rows_z = density.shape
    blk_start = lax.axis_index("blk") * rows_y
    sub_start = lax.axis_index("sub") * rows_z
    field = jnp.zeros((rows_x, rows_y, rows_z), jnp.float32)
    for factor, (dim_x, dim_y, dim_z) in enumerate(level_dims()):
        extended = jnp.concatenate([slabs[factor], after[factor]], axis=0)
        mat_x = local_hat(rows_x, dim_x // slab_count + 1, dim_x)
        mat_y = hat_matrix(FINE_Y, dim_y, blk_start, rows_y)
        mat_z = hat_matrix(FINE_Z, dim_z, sub_start, rows_z)
        field = field + level_amplitude[factor] * interpolate(mat_x, mat_y, mat_z, extended)
    total = by_axis(jnp.sum(density * field), ("slab", "blk", "sub"))
    energy = (total / (FINE_X * FINE_Y * FINE_Z)).reshape(1)
    return (field, energy)


def solution(mesh):
    in_specs = (
        P(("grp", "slab", "blk", "sub")),
        P(("grp", "slab", "blk", "sub")),
        P(("grp", "slab", "blk", "sub")),
        P(None, ("grp", "slab", "blk", "sub")),
        P(("grp", "slab", "blk", "sub")),
        P(("grp", "slab", "blk", "sub")),
        P(),
        P(("grp", "slab"), "blk", "sub"),
    )
    out_specs = (P(("grp", "slab"), "blk", "sub"), P("grp"))
    return jax.shard_map(
        on_device, mesh=mesh, in_specs=in_specs, out_specs=out_specs, check_vma=False
    )
```

profile of v0, /device:TPU:33, one launch (start us, length us, event | category | flops | bytes accessed | tf_op | source)
XLA Modules:
  0.0 214.6 jit_solution(13088567531267280203)
XLA Ops:
  7.3 0.8 fusion.396
  8.7 0.7 convert_add_fusion.2
  9.4 0.7 convert_add_fusion.1
  10.1 0.7 convert_add_fusion
  10.8 0.7 compare_select_fusion
  11.5 42.4 %all_gather.27 = f32[4096,4]{0,1:T(4,128)S(1)} all-gather(f32[256,4]{0,1:T(4,128)S(1)} %pad_maximum_fusion), channel_id=1, replica_groups=mesh['grp'=2,'slab'=16,'blk'=4,'sub'=2] {'slab'}, dimensions={0}, use_global_device_ids=true | all-gather | bytes 69632 | tf_op jit(solution)/shard_map/all_gather | solution.py:20
  54.0 35.3 %while.22 = (s32[]{:T(128)}, f32[512,128]{1,0:T(8,128)S(1)}, f32[288,96]{1,0:T(8,128)S(1)}, f32[128,64]{0,1:T(8,128)S(1)}, f32[32,32]{1,0:T(8,128)S(1)}, /*index...) while((s32[]{:T(128)}, f32[512,128]{1,0:T(8,128)S(1)}, ...), condition=%wide.region_1.0_spmd.clone, body=%wide.region_0.0_spmd.clone.sunk | while | flops 54709520 | bytes 2422072 | solution.py:139
  54.6 0.3 multiply_convert_fusion.10
  54.9 0.4 convolution_add_fusion.8
  56.8 0.3 multiply_convert_fusion.10
  57.1 0.4 convolution_add_fusion.8
  57.7 0.2 convolution_add_fusion.9
  59.0 0.3 multiply_convert_fusion.10
  59.3 0.4 convolution_add_fusion.8
  61.2 0.3 multiply_convert_fusion.10
  61.5 0.4 convolution_add_fusion.8
  63.4 0.3 multiply_convert_fusion.10
  63.8 0.4 convolution_add_fusion.8
  65.6 0.3 multiply_convert_fusion.10
  66.0 0.4 convolution_add_fusion.8
  67.8 0.3 multiply_convert_fusion.10
  68.2 0.4 convolution_add_fusion.8
  70.0 0.3 multiply_convert_fusion.10
  70.4 0.4 convolution_add_fusion.8
  72.2 0.3 multiply_convert_fusion.10
  72.6 0.4 convolution_add_fusion.8
  74.4 0.3 multiply_convert_fusion.10
  74.8 0.4 convolution_add_fusion.8
  76.6 0.3 multiply_convert_fusion.10
  77.0 0.4 convolution_add_fusion.8
  78.9 0.3 multiply_convert_fusion.10
  79.2 0.4 convolution_add_fusion.8
  81.1 0.3 multiply_convert_fusion.10
  81.4 0.4 convolution_add_fusion.8
  83.3 0.3 multiply_convert_fusion.10
  83.6 0.4 convolution_add_fusion.8
  85.5 0.3 multiply_convert_fusion.10
  85.8 0.4 convolution_add_fusion.8
  87.7 0.3 multiply_convert_fusion.10
  88.0 0.4 convolution_add_fusion.8
  89.3 0.7 copy-done.1
  90.1 23.4 %all-gather.1 = f32[2304,96]{1,0:T(8,128)S(1)} all-gather(f32[288,96]{1,0:T(8,128)S(1)} %get-tuple-element.257), channel_id=3, replica_groups=mesh['grp'=2,'slab'=16,'blk'=4,'sub'=2] {'blk','sub'}, dimensions={0}, use_global_device_ids=true | all-gather | bytes 995328 | tf_op jit(solution)/shard_map/all_gather | solution.py:29
  113.8 13.0 %all-gather.3 = f32[256,32]{1,0:T(8,128)S(1)} all-gather(f32[32,32]{1,0:T(8,128)S(1)} %get-tuple-element.259), channel_id=5, replica_groups=mesh['grp'=2,'slab'=16,'blk'=4,'sub'=2] {'blk','sub'}, dimensions={0}, use_global_device_ids=true | all-gather | bytes 36864 | tf_op jit(solution)/shard_map/all_gather | solution.py:29
  126.9 13.1 %all-gather.2 = f32[1024,64]{0,1:T(8,128)S(1)} all-gather(f32[128,64]{0,1:T(8,128)S(1)} %get-tuple-element.258), channel_id=4, replica_groups=mesh['grp'=2,'slab'=16,'blk'=4,'sub'=2] {'blk','sub'}, dimensions={0}, use_global_device_ids=true | all-gather | bytes 294912 | tf_op jit(solution)/shard_map/all_gather | solution.py:29
  140.2 0.3 collective-permute-start.2
  140.6 0.6 fusion.397
  141.6 0.5 fusion.144
  142.1 0.6 convolution_bitcast_fusion.3
  142.8 1.7 convolution_multiply_fusion
  144.4 0.7 fusion.87
  145.2 1.1 convolution_bitcast_fusion
  146.2 1.0 fusion.83
  147.2 1.7 reduce_sum.45
  149.0 1.2 collective-permute-start
  150.1 0.9 convolution_bitcast_fusion.1
  151.2 1.8 collective-permute-done
  153.1 1.2 fusion.77
  154.2 1.0 convolution_bitcast_fusion.2
  155.3 1.3 convolution_multiply_fusion.3
  156.6 1.3 fusion.74
  157.9 3.1 %multiply_reduce_fusion = (f32[]{:T(128)}, f32[16,64,128]{2,1,0:T(8,128)}) fusion(f32[16,64,128]{2,1,0:T(8,128)S(1)} %copy-done, f32[16,64,128]{2,1,0:T(8,128)S(1)} %convolution_multiply_fusion, f32[16,64,128]{2,1,0:T(8,128)S(1)} %fusion.74, f32[16,64,64]{1,2,0:T(8,128)S(1)} %convolution_bitcast_fusion, s32[128]{0:T(128)S(1)} %fusion.309, ...), kind=kOutput, calls=%fused_computation.123 | convolution fusion | flops 101490688 | bytes 2360072 | tf_op jit(solution)/shard_map/cz,abz->abc/dot_general | solution.py:111
  161.0 23.5 %psum.21 = f32[]{:T(128)} all-reduce(f32[]{:T(128)} %get-tuple-element.354), channel_id=1, replica_groups=mesh['grp'=2,'slab'=16,'blk'=4,'sub'=2] {'slab'}, use_global_device_ids=true, to_apply=%region_7.8 | all-reduce | flops 1 | bytes 8 | tf_op jit(solution)/shard_map/psum | solution.py:38
  184.5 8.1 %psum.22 = f32[]{:T(128)} all-reduce(f32[]{:T(128)} %psum.21), channel_id=1, replica_groups=mesh['grp'=2,'slab'=16,'blk'=4,'sub'=2] {'blk'}, use_global_device_ids=true, to_apply=%region_8.9 | all-reduce | flops 1 | bytes 8 | tf_op jit(solution)/shard_map/psum | solution.py:38
  192.6 13.3 %psum.23 = f32[]{:T(128)} all-reduce(f32[]{:T(128)} %psum.22), channel_id=1, replica_groups=mesh['grp'=2,'slab'=16,'blk'=4,'sub'=2] {'sub'}, use_global_device_ids=true, to_apply=%region_9.10 | all-reduce | flops 1 | bytes 8 | tf_op jit(solution)/shard_map/psum | solution.py:38
  (366 shorter events, 23.7 us)
Async XLA Ops:
  7.2 140.1 %all-gather.6.cloned.1.call-start = ((), (), s32[]{:S(2)}) async-start(), calls=%async_computation | async-start | bytes 2359296 | tf_op jit(solution)/shard_map/all_gather | solution.py:29
  89.3 0.7 copy-start.1
  90.1 50.5 %copy-start.2 = (f32[4]{0:T(128)S(1)}, f32[4]{0:T(128)}, u32[]{:S(2)}) copy-start(f32[4]{0:T(128)} %param.16) | copy-start | bytes 52
  113.6 32.6 %collective-permute-start.1 = (f32[1,96,96]{2,0,1:T(1,128)S(1)}, f32[1,96,96]{2,0,1:T(1,128)S(1)}, u32[]{:S(2)}, u32[]{:S(2)}) collective-permute-start(f32[1,96,96]{2,0,1:T(1,128)S(1)} %bitcast.118), channel_id=1, source_target_pairs={{0,120},{8,0},{16,8},{24,16},{32,24},{40,32},{48,40},{56,48},{64,5... | collective-permute-start | bytes 110600 | tf_op jit(solution)/shard_map/ppermute | solution.py:34
  126.7 14.8 %collective-permute-start.3 = (f32[1,32,32]{2,0,1:T(1,128)S(1)}, f32[1,32,32]{2,0,1:T(1,128)S(1)}, u32[]{:S(2)}, u32[]{:S(2)}) collective-permute-start(f32[1,32,32]{2,0,1:T(1,128)S(1)} %bitcast.115), channel_id=1, source_target_pairs={{0,120},{8,0},{16,8},{24,16},{32,24},{40,32},{48,40},{56,48},{64,5... | collective-permute-start | bytes 12296 | tf_op jit(solution)/shard_map/ppermute | solution.py:34
  140.2 4.3 %collective-permute-start.2 = (f32[1,64,64]{2,0,1:T(1,128)S(1)}, f32[1,64,64]{2,0,1:T(1,128)S(1)}, u32[]{:S(2)}, u32[]{:S(2)}) collective-permute-start(f32[1,64,64]{2,0,1:T(1,128)S(1)} %bitcast.119), channel_id=1, source_target_pairs={{0,120},{8,0},{16,8},{24,16},{32,24},{40,32},{48,40},{56,48},{64,5... | collective-permute-start | bytes 49160 | tf_op jit(solution)/shard_map/ppermute | solution.py:34
  149.0 4.1 %collective-permute-start = (f32[1,128,128]{2,0,1:T(1,128)S(1)}, f32[1,128,128]{2,0,1:T(1,128)S(1)}, u32[]{:S(2)}, u32[]{:S(2)}) collective-permute-start(f32[1,128,128]{2,0,1:T(1,128)S(1)} %bitcast.117), channel_id=1, source_target_pairs={{0,120},{8,0},{16,8},{24,16},{32,24},{40,32},{48,40},{56,48},{64,5... | collective-permute-start | bytes 196616 | tf_op jit(solution)/shard_map/ppermute | solution.py:34
  154.2 3.6 %copy-start = (f32[16,64,128]{2,1,0:T(8,128)S(1)}, f32[16,64,128]{2,1,0:T(8,128)}, u32[]{:S(2)}) copy-start(f32[16,64,128]{2,1,0:T(8,128)} %param.17) | copy-start | bytes 1572868
Sparse Core Ops, SparseCore 0:
  90.2 32.4 all-gather.5
where the time goes:
time: 215 us
  blocking collectives  137 us (64%)
  matrix products  28.8 us (13%)
  other arithmetic  21.5 us (10%)
  between operations  16.9 us (8%)
  local copies, waits for them, and re-layouts  5.18 us (2%)
    all_gather x3, blocking collectives, over_pieces(): return lax.all_gather(value, axis).sum(0)  49.4 us
    psum x3, blocking collectives, by_axis(): return functools.reduce(lax.psum, axes, value)  44.9 us
    all_gather x1, blocking collectives, rows_first(): out, at, gathered = (lax.all_gather(both, axis, axis=0, tiled=True), 0, [])  42.4 us
    dot_general x64, matrix products, spread_slab(): lax.dot_general(planes, along_z.astype(jnp.bfloat16), (((0,), (0,)), ((),...  14.4 us
    dot_general x4, matrix products, interpolate(): return jnp.einsum('cz,abz->abc', mat_z, second, precision=highest)  7.4 us
    convert_element_type x48, other arithmetic, spread_slab(): planes = ((weighted[:, None] * along_x)[:, :, None] * along_y[:, None, :]...  5.89 us
    mul x64, other arithmetic, spread_slab(): weighted[:, None] * along_x  5.47 us
  transfers between devices with their start and end apart: 5, of which 1 were waited for; matrix products, arithmetic and copies ran while one was open for 4% of the time, Pallas kernels for 0%

commit v1 on v0

--- a/solution.py
+++ b/solution.py
@@ -17,7 +17,13 @@
 def rows_first(arrays, axis, dims):
     turned = [jnp.moveaxis(a, dim, 0) for a, dim in zip(arrays, dims)]
     both = jnp.concatenate([t.reshape(len(t), -1) for t in turned], axis=1)
-    out, at, gathered = (lax.all_gather(both, axis, axis=0, tiled=True), 0, [])
+    out, at, gathered = (
+        jnp.concatenate(
+            lax.all_to_all(jnp.stack([both] * lax.axis_size(axis)), axis, 0, 0), axis=0
+        ),
+        0,
+        [],
+    )
     for t, dim in zip(turned, dims):
         share = out[:, at : at + t[0].size].reshape(-1, *t.shape[1:])
         gathered.append(jnp.moveaxis(share, 0, dim))

time: 215 us -> 205 us (0.953)
  blocking collectives: 137 us -> 91.3 us
  starting transfers between devices: 1.76 us -> 26.4 us
  waiting for transfers between devices: 1.9 us -> 12.2 us
    all_gather x1 -> x0, blocking collectives: 42.4 us -> none  [rows_first(): out, at, gathered = (lax.all_gather(both, axis, axis=0, tiled=True), 0, [])]
    all_to_all x0 -> x1, starting transfers between devices: none -> 24.5 us  [rows_first(): lax.all_to_all(jnp.stack([both] * lax.axis_size(axis)), axis, 0, 0)]
    all_to_all x0 -> x1, waiting for transfers between devices: none -> 11.2 us  [rows_first(): lax.all_to_all(jnp.stack([both] * lax.axis_size(axis)), axis, 0, 0)]
    all_gather x3, blocking collectives: 49.4 us -> 44.9 us  [over_pieces(): return lax.all_gather(value, axis).sum(0)]
  transfers between devices with their start and end apart: 5 -> 6, of which waited for: 1 -> 2; matrix products, arithmetic and copies ran while one was open for 4% -> 4% of each run, Pallas kernels for 0% -> 0%
where the time goes in v1:
time: 205 us
  blocking collectives  91.3 us (45%)
  matrix products  28.7 us (14%)
  starting transfers between devices  26.4 us (13%)
  other arithmetic  21.5 us (10%)
  between operations  16.9 us (8%)
  waiting for transfers between devices  12.2 us (6%)
  local copies, waits for them, and re-layouts  5.84 us (3%)
    psum x3, blocking collectives, by_axis(): return functools.reduce(lax.psum, axes, value)  46.4 us
    all_gather x3, blocking collectives, over_pieces(): return lax.all_gather(value, axis).sum(0)  44.9 us
    all_to_all x1, starting transfers between devices, rows_first(): lax.all_to_all(jnp.stack([both] * lax.axis_size(axis)), axis, 0, 0)  24.5 us
    dot_general x64, matrix products, spread_slab(): lax.dot_general(planes, along_z.astype(jnp.bfloat16), (((0,), (0,)), ((),...  14.4 us
    all_to_all x1, waiting for transfers between devices, rows_first(): lax.all_to_all(jnp.stack([both] * lax.axis_size(axis)), axis, 0, 0)  11.2 us
    dot_general x4, matrix products, interpolate(): return jnp.einsum('cz,abz->abc', mat_z, second, precision=highest)  7.28 us
    convert_element_type x48, other arithmetic, spread_slab(): planes = ((weighted[:, None] * along_x)[:, :, None] * along_y[:, None, :]...  5.89 us
    mul x64, other arithmetic, spread_slab(): weighted[:, None] * along_x  5.47 us
  transfers between devices with their start and end apart: 6, of which 2 were waited for; matrix products, arithmetic and copies ran while one was open for 4% of the time, Pallas kernels for 0%

profile of v1, /device:TPU:33, one launch (start us, length us, event | category | flops | bytes accessed | tf_op | source)
XLA Modules:
  0.0 204.6 jit_solution(16818861436442328595)
XLA Ops:
  7.2 0.8 fusion.396
  8.6 0.7 convert_add_fusion.2
  9.3 0.7 convert_add_fusion.1
  10.0 0.7 convert_add_fusion
  10.7 0.7 compare_select_fusion
  11.4 0.6 stack.2
  12.0 24.5 %all-to-all-start = ((f32[16,256,4]{1,2,0:T(4,128)}), f32[16,256,4]{1,2,0:T(4,128)S(1)}, u32[]{:S(2)}, u32[]{:S(2)}) async-start(f32[16,256,4]{1,2,0:T(4,128)} %stack.2), calls=%async_computation | async-start | bytes 131072 | tf_op jit(solution)/shard_map/all_to_all | solution.py:22
  36.7 11.2 %all-to-all-done = f32[16,256,4]{1,2,0:T(4,128)S(1)} async-done(((f32[16,256,4]{1,2,0:T(4,128)}), f32[16,256,4]{1,2,0:T(4,128)S(1)}, u32[]{:S(2)}, u32[]{:S(2)}) %all-to-all-start) | async-done | bytes 65568 | tf_op jit(solution)/shard_map/all_to_all | solution.py:22
  48.0 35.3 %while.22 = (s32[]{:T(128)}, f32[512,128]{1,0:T(8,128)S(1)}, f32[288,96]{1,0:T(8,128)S(1)}, f32[128,64]{0,1:T(8,128)S(1)}, f32[32,32]{1,0:T(8,128)S(1)}, /*index...) while((s32[]{:T(128)}, f32[512,128]{1,0:T(8,128)S(1)}, ...), condition=%wide.region_1.0_spmd.clone, body=%wide.region_0.0_spmd.clone.sunk | while | flops 54709520 | bytes 2422072 | solution.py:145
  48.5 0.3 multiply_convert_fusion.10
  48.9 0.4 convolution_add_fusion.8
  50.8 0.3 multiply_convert_fusion.10
  51.1 0.4 convolution_add_fusion.8
  53.0 0.3 multiply_convert_fusion.10
  53.3 0.4 convolution_add_fusion.8
  55.2 0.3 multiply_convert_fusion.10
  55.5 0.4 convolution_add_fusion.8
  57.4 0.3 multiply_convert_fusion.10
  57.7 0.4 convolution_add_fusion.8
  59.6 0.3 multiply_convert_fusion.10
  59.9 0.4 convolution_add_fusion.8
  61.8 0.3 multiply_convert_fusion.10
  62.1 0.4 convolution_add_fusion.8
  64.0 0.3 multiply_convert_fusion.10
  64.3 0.4 convolution_add_fusion.8
  66.2 0.3 multiply_convert_fusion.10
  66.5 0.4 convolution_add_fusion.8
  68.4 0.3 multiply_convert_fusion.10
  68.7 0.4 convolution_add_fusion.8
  70.6 0.3 multiply_convert_fusion.10
  71.0 0.4 convolution_add_fusion.8
  72.8 0.3 multiply_convert_fusion.10
  73.2 0.4 convolution_add_fusion.8
  75.0 0.3 multiply_convert_fusion.10
  75.4 0.4 convolution_add_fusion.8
  77.2 0.3 multiply_convert_fusion.10
  77.6 0.4 convolution_add_fusion.8
  79.4 0.3 multiply_convert_fusion.10
  79.8 0.4 convolution_add_fusion.8
  81.6 0.3 multiply_convert_fusion.10
  82.0 0.4 convolution_add_fusion.8
  83.3 0.7 copy-done.1
  84.2 0.6 fusion.397
  84.9 17.9 %all-gather.1 = f32[2304,96]{1,0:T(8,128)S(1)} all-gather(f32[288,96]{1,0:T(8,128)S(1)} %get-tuple-element.257), channel_id=3, replica_groups=mesh['grp'=2,'slab'=16,'blk'=4,'sub'=2] {'blk','sub'}, dimensions={0}, use_global_device_ids=true | all-gather | bytes 995328 | tf_op jit(solution)/shard_map/all_gather | solution.py:35
  103.2 13.7 %all-gather.3 = f32[256,32]{1,0:T(8,128)S(1)} all-gather(f32[32,32]{1,0:T(8,128)S(1)} %get-tuple-element.259), channel_id=5, replica_groups=mesh['grp'=2,'slab'=16,'blk'=4,'sub'=2] {'blk','sub'}, dimensions={0}, use_global_device_ids=true | all-gather | bytes 36864 | tf_op jit(solution)/shard_map/all_gather | solution.py:35
  117.0 13.3 %all-gather.2 = f32[1024,64]{0,1:T(8,128)S(1)} all-gather(f32[128,64]{0,1:T(8,128)S(1)} %get-tuple-element.258), channel_id=4, replica_groups=mesh['grp'=2,'slab'=16,'blk'=4,'sub'=2] {'blk','sub'}, dimensions={0}, use_global_device_ids=true | all-gather | bytes 294912 | tf_op jit(solution)/shard_map/all_gather | solution.py:35
  131.0 0.5 fusion.144
  131.6 0.6 convolution_bitcast_fusion.3
  132.2 1.7 convolution_multiply_fusion
  133.9 0.7 fusion.87
  134.6 1.1 convolution_bitcast_fusion
  135.7 1.0 fusion.83
  136.7 1.7 reduce_sum.45
  138.4 1.2 collective-permute-start
  139.7 0.9 convolution_bitcast_fusion.1
  140.7 0.9 collective-permute-done
  141.7 1.2 fusion.77
  142.8 1.0 convolution_bitcast_fusion.2
  143.9 1.2 convolution_multiply_fusion.3
  145.1 1.3 fusion.74
  146.4 3.1 %multiply_reduce_fusion = (f32[]{:T(128)}, f32[16,64,128]{2,1,0:T(8,128)}) fusion(f32[16,64,128]{2,1,0:T(8,128)S(1)} %copy-done, f32[16,64,128]{2,1,0:T(8,128)S(1)} %convolution_multiply_fusion, f32[16,64,128]{2,1,0:T(8,128)S(1)} %fusion.74, f32[16,64,64]{1,2,0:T(8,128)S(1)} %convolution_bitcast_fusion, s32[128]{0:T(128)S(1)} %fusion.309, ...), kind=kOutput, calls=%fused_computation.123 | convolution fusion | flops 101490688 | bytes 2360072 | tf_op jit(solution)/shard_map/cz,abz->abc/dot_general | solution.py:117
  149.5 23.8 %psum.21 = f32[]{:T(128)} all-reduce(f32[]{:T(128)} %get-tuple-element.354), channel_id=1, replica_groups=mesh['grp'=2,'slab'=16,'blk'=4,'sub'=2] {'slab'}, use_global_device_ids=true, to_apply=%region_7.8 | all-reduce | flops 1 | bytes 8 | tf_op jit(solution)/shard_map/psum | solution.py:44
  173.3 8.6 %psum.22 = f32[]{:T(128)} all-reduce(f32[]{:T(128)} %psum.21), channel_id=1, replica_groups=mesh['grp'=2,'slab'=16,'blk'=4,'sub'=2] {'blk'}, use_global_device_ids=true, to_apply=%region_8.9 | all-reduce | flops 1 | bytes 8 | tf_op jit(solution)/shard_map/psum | solution.py:44
  182.0 14.0 %psum.23 = f32[]{:T(128)} all-reduce(f32[]{:T(128)} %psum.22), channel_id=1, replica_groups=mesh['grp'=2,'slab'=16,'blk'=4,'sub'=2] {'sub'}, use_global_device_ids=true, to_apply=%region_9.10 | all-reduce | flops 1 | bytes 8 | tf_op jit(solution)/shard_map/psum | solution.py:44
  (368 shorter events, 24.3 us)
Async XLA Ops:
  12.0 35.9 %all-to-all-start = ((f32[16,256,4]{1,2,0:T(4,128)}), f32[16,256,4]{1,2,0:T(4,128)S(1)}, u32[]{:S(2)}, u32[]{:S(2)}) async-start(f32[16,256,4]{1,2,0:T(4,128)} %stack.2), calls=%async_computation | async-start | bytes 131072 | tf_op jit(solution)/shard_map/all_to_all | solution.py:22
  36.5 100.1 %all-gather.6.cloned.1.call-start = ((), (), s32[]{:S(2)}) async-start(), calls=%async_computation.1 | async-start | bytes 2359296 | tf_op jit(solution)/shard_map/all_gather | solution.py:35
  48.0 36.3 %copy-start.2 = (f32[4]{0:T(128)S(1)}, f32[4]{0:T(128)}, u32[]{:S(2)}) copy-start(f32[4]{0:T(128)} %param.16) | copy-start | bytes 52
  83.3 0.7 copy-start.1
  103.0 32.7 %collective-permute-start.1 = (f32[1,96,96]{2,0,1:T(1,128)S(1)}, f32[1,96,96]{2,0,1:T(1,128)S(1)}, u32[]{:S(2)}, u32[]{:S(2)}) collective-permute-start(f32[1,96,96]{2,0,1:T(1,128)S(1)} %bitcast.120), channel_id=1, source_target_pairs={{0,120},{8,0},{16,8},{24,16},{32,24},{40,32},{48,40},{56,48},{64,5... | collective-permute-start | bytes 110600 | tf_op jit(solution)/shard_map/ppermute | solution.py:40
  116.9 14.1 %collective-permute-start.3 = (f32[1,32,32]{2,0,1:T(1,128)S(1)}, f32[1,32,32]{2,0,1:T(1,128)S(1)}, u32[]{:S(2)}, u32[]{:S(2)}) collective-permute-start(f32[1,32,32]{2,0,1:T(1,128)S(1)} %bitcast.117), channel_id=1, source_target_pairs={{0,120},{8,0},{16,8},{24,16},{32,24},{40,32},{48,40},{56,48},{64,5... | collective-permute-start | bytes 12296 | tf_op jit(solution)/shard_map/ppermute | solution.py:40
  130.7 3.1 %collective-permute-start.2 = (f32[1,64,64]{2,0,1:T(1,128)S(1)}, f32[1,64,64]{2,0,1:T(1,128)S(1)}, u32[]{:S(2)}, u32[]{:S(2)}) collective-permute-start(f32[1,64,64]{2,0,1:T(1,128)S(1)} %bitcast.121), channel_id=1, source_target_pairs={{0,120},{8,0},{16,8},{24,16},{32,24},{40,32},{48,40},{56,48},{64,5... | collective-permute-start | bytes 49160 | tf_op jit(solution)/shard_map/ppermute | solution.py:40
  138.4 3.2 %collective-permute-start = (f32[1,128,128]{2,0,1:T(1,128)S(1)}, f32[1,128,128]{2,0,1:T(1,128)S(1)}, u32[]{:S(2)}, u32[]{:S(2)}) collective-permute-start(f32[1,128,128]{2,0,1:T(1,128)S(1)} %bitcast.119), channel_id=1, source_target_pairs={{0,120},{8,0},{16,8},{24,16},{32,24},{40,32},{48,40},{56,48},{64,5... | collective-permute-start | bytes 196616 | tf_op jit(solution)/shard_map/ppermute | solution.py:40
  142.8 3.6 %copy-start = (f32[16,64,128]{2,1,0:T(8,128)S(1)}, f32[16,64,128]{2,1,0:T(8,128)}, u32[]{:S(2)}) copy-start(f32[16,64,128]{2,1,0:T(8,128)} %param.17) | copy-start | bytes 1572868
Sparse Core Ops, SparseCore 0:
  84.2 26.9 all-gather.5
